TPU v7x, 32 devices: a whole 2x2x4 slice. The times are simulated.
32 devices in a mesh: net: 4 (over y, x), line: 8 (over z, core).
Axes of the slice: x: 2, y: 2, z: 4, core: 2. Of those that a mesh axis runs over, the one named last changes fastest.
Arguments:
- conductance_inverse: float32 [4, 4096, 4096], P('net', 'line'), may hold values from -0.5 to 4.5, as said below
- prior_voltage: float32 [4, 96, 4096], P('net', None, 'line'), may hold values from -6 to 6
- sources: float32 [3, 4, 4096], P(None, 'net', 'line'), may hold values from -6 to 6
- fault_node: int32 [96], replicated, may hold values from 0 to 16383
- fault_conductance: float32 [96], replicated, may hold values from 0.5 to 4
- terminal_node: int32 [4, 3, 4096], P('net', None, 'line'), may hold values from 0 to 4095
- ownership: int32 [4, 4096], P('net', 'line'), may hold values from 0 to 1, as said below
- partner: int32 [4, 4096], P('net', 'line'), may hold values from 0 to 31, as said below
- delay_steps: int32 [4, 4096], P('net', 'line'), may hold values from 1 to 4, as said below
- surge_conductance: float32 [4, 4096], P('net', 'line'), may hold values from 0.2 to 1
- pole_wave: float32 [4, 6, 4096], P('net', None, 'line'), may hold values from 0.2 to 0.95
- residue_wave: float32 [4, 6, 3, 3, 4096], P('net', None, None, None, 'line'), may hold values from -1 to 1
- pole_admit: float32 [4, 6, 4096], P('net', None, 'line'), may hold values from 0.2 to 0.95
- residue_admit: float32 [4, 6, 3, 3, 4096], P('net', None, None, None, 'line'), may hold values from -1 to 1
- wave_state: float32 [4, 6, 3, 96, 4096], P('net', None, None, None, 'line'), may hold values from -4 to 4
- admit_state: float32 [4, 6, 3, 96, 4096], P('net', None, None, None, 'line'), may hold values from -4 to 4
- wave_history: float32 [4, 4, 3, 96, 4096], P('net', None, None, None, 'line'), may hold values from -6 to 6
Outputs:
- final_voltage: float32 [4, 96, 4096], P('net', None, 'line')
- end_current: float32 [4, 3, 96, 4096], P('net', None, None, 'line')
Inputs may be any that keep to these rules, and one draw needn't show every extreme that they name: `conductance_inverse`: each block is exactly symmetric. `ownership`: A slot is live exactly when the slot of the same number j % 512 at its partner owner is live; the number of live slots differs from owner to owner. The far end of slot j lies in the slot of the same number j % 512 at the partner owner, the partner of that slot is the first owner again, never the owner itself, and at most 17 live slots of one owner have the same partner; this many occur. `delay_steps`: equal at both ends of a line.
All inputs are finite; a program needn't handle non-finite values.
Results may differ from a plain program's by a relative error of at most 0.0003.
Values sent between devices are 32-bit elements; how exact they have to be, the bound alone decides.
A program may use at most 128 MiB of HBM per device.

v0:
```python
import jax
import jax.numpy as jnp
from jax import lax
from jax.sharding import PartitionSpec as P

STEPS = 3


def mix_residue(residue, vector):
    return (
        residue[:, :, 0, None, :] * vector[0]
        + residue[:, :, 1, None, :] * vector[1]
        + residue[:, :, 2, None, :] * vector[2]
    )


def select_delayed(buffer, delay_local):
    depth_count = buffer.shape[0]
    chosen = delay_local[None, :] == jnp.arange(1, depth_count + 1, dtype=jnp.int32)[:, None]
    return jnp.sum(jnp.where(chosen[:, None, None, :], buffer, 0.0), axis=0)


def terminal_values(voltage, terminal):
    picked = jnp.take(voltage, terminal.reshape(-1), axis=1)
    return jnp.moveaxis(picked.reshape(voltage.shape[0], 3, -1), 0, 1)


def spread_ends(history, terminal, node_count):
    values = jnp.moveaxis(history, 0, 1).reshape(history.shape[1], -1)
    return (
        jnp.zeros((history.shape[1], node_count), jnp.float32)
        .at[:, terminal.reshape(-1)]
        .add(values)
    )


def gather_full(block):
    return lax.all_gather(block, "line", axis=1, tiled=True)


def on_device(
    conductance_inverse,
    prior_voltage,
    sources,
    fault_node,
    fault_conductance,
    terminal_node,
    ownership,
    partner,
    delay_steps,
    surge_conductance,
    pole_wave,
    residue_wave,
    pole_admit,
    residue_admit,
    wave_state,
    admit_state,
    wave_history,
):
    inverse_block = conductance_inverse[0]
    row_count = inverse_block.shape[0]
    node_count = inverse_block.shape[1]
    line_index = lax.axis_index("line")
    net_index = lax.axis_index("net")
    offset = line_index * row_count
    net_count = lax.axis_size("net")
    line_count = lax.axis_size("line")
    devices = net_count * line_count
    slot_count = ownership.shape[1]
    capacity = (slot_count + devices - 2) // (devices - 1)
    is_live = ownership[0] > 0
    live_float = is_live.astype(jnp.float32)
    terminal = terminal_node[0]
    delay_local = delay_steps[0]
    surge_local = surge_conductance[0]
    partners = partner[0]
    slot_range = jnp.arange(slot_count, dtype=jnp.int32)
    earlier = (
        (partners[:, None] == partners[None, :])
        & is_live[None, :]
        & (slot_range[None, :] < slot_range[:, None])
    )
    slot_rank = jnp.sum(earlier.astype(jnp.int32), axis=1)
    position = jnp.where(is_live, partners * capacity + slot_rank, devices * capacity)
    scenario_range = jnp.arange(prior_voltage.shape[1], dtype=jnp.int32)
    fault_sub = fault_node // node_count
    fault_local = fault_node % node_count
    fault_here = (fault_sub == net_index) & (fault_local // row_count == line_index)
    wave_decay = pole_wave[0][:, None, None, :]
    admit_decay = pole_admit[0][:, None, None, :]
    wave_res = residue_wave[0]
    admit_res = residue_admit[0]
    voltage = gather_full(prior_voltage[0])
    voltage_rows = prior_voltage[0]
    wave_now = wave_state[0]
    admits = admit_state[0]
    history_buffer = wave_history[0]
    outgoing = None
    current = None
    for step_index in range(STEPS):
        terminal_prior = terminal_values(voltage, terminal)
        admits = admit_decay * admits + mix_residue(admit_res, terminal_prior)
        if step_index == 0:
            wave_now = wave_decay * wave_now + mix_residue(
                wave_res, select_delayed(history_buffer, delay_local)
            )
        else:
            shifted = jnp.concatenate(
                [jnp.zeros_like(history_buffer[:1]), history_buffer[:-1]], axis=0
            )
            wave_now = wave_decay * wave_now + mix_residue(
                wave_res, select_delayed(shifted, delay_local)
            )
            row_width = outgoing.shape[0] * outgoing.shape[1]
            packed = jnp.moveaxis(outgoing, 2, 0).reshape(slot_count, row_width)
            buffer = (
                jnp.zeros((devices * capacity, row_width), jnp.float32)
                .at[position]
                .set(packed, mode="drop")
            )
            arrived = lax.all_to_all(
                buffer, ("net", "line"), split_axis=0, concat_axis=0, tiled=True
            )
            picked_rows = arrived[jnp.minimum(position, devices * capacity - 1)]
            arrived = jnp.moveaxis(picked_rows.reshape(slot_count, 3, -1), 0, 2) * live_float
            newest = jnp.where((delay_local == 1)[None, None, :], arrived, 0.0)
            wave_now = wave_now + mix_residue(wave_res, newest)
            history_buffer = jnp.concatenate([arrived[None], shifted[1:]], axis=0)
        history = (jnp.sum(wave_now, axis=0) - jnp.sum(admits, axis=0)) * live_float
        injection = spread_ends(history, terminal, node_count)
        own_part = (
            lax.dynamic_slice_in_dim(injection, offset, row_count, 1)
            + sources[step_index, 0][None, :]
        )
        injection = lax.dynamic_update_slice_in_dim(injection, own_part, offset, 1)
        fault_value = voltage[scenario_range, fault_local]
        injection = injection.at[scenario_range, fault_local].add(
            jnp.where(fault_here, -fault_conductance * fault_value, 0.0)
        )
        summed = lax.psum(injection, "line")
        voltage_rows = lax.dot_general(
            summed,
            inverse_block,
            (((1,), (1,)), ((), ())),
            precision=lax.Precision.HIGHEST,
            preferred_element_type=jnp.float32,
        )
        voltage = gather_full(voltage_rows)
        terminal_now = terminal_values(voltage, terminal)
        if step_index + 1 < STEPS:
            outgoing = (2.0 * surge_local * terminal_now - history) * live_float
        else:
            current = (surge_local * terminal_now - history) * live_float
    return (voltage_rows[None], current[None])


def solution(mesh):
    return jax.shard_map(
        on_device,
        mesh=mesh,
        in_specs=(
            P("net", "line", None),
            P("net", None, "line"),
            P(None, "net", "line"),
            P(),
            P(),
            P("net", None, "line"),
            P("net", "line"),
            P("net", "line"),
            P("net", "line"),
            P("net", "line"),
            P("net", None, "line"),
            P("net", None, None, None, "line"),
            P("net", None, "line"),
            P("net", None, None, None, "line"),
            P("net", None, None, None, "line"),
            P("net", None, None, None, "line"),
            P("net", None, None, None, "line"),
        ),
        out_specs=(P("net", None, "line"), P("net", None, None, "line")),
        check_vma=False,
    )
```

profile of v0, /device:TPU:0, one launch (start us, length us, event | category | flops | bytes accessed | tf_op | source)
XLA Modules:
  0.0 578.2 jit_solution(13432879487147559588)
XLA Ops:
  32.9 8.7 %all-gather.12.cloned.1.call-done = f32[1,96,4096]{1,2,0:T(8,128)} async-done(((f32[1,96,512]{1,2,0:T(8,128)}), f32[1,96,4096]{1,2,0:T(8,128)}) %all-gather.12.cloned.1.call-update) | async-done | bytes 1572880 | tf_op jit(solution)/shard_map/all_gather | solution.py:38
  41.5 3.6 gather_fusion
  45.1 5.6 gather_fusion.5
  64.8 10.5 %scatter_custom_fusion = f32[96,4096]{0,1:T(8,128)} fusion(s32[1536]{0:T(1024)} %fusion.32, f32[1536,96]{1,0:T(8,128)} %copy.74, f32[]{:T(128)} %constant.37.clone.1), kind=kCustom, calls=%fused_computation.47 | custom fusion | flops 147456 | bytes 1573376 | tf_op jit(solution)/shard_map/scatter-add | solution.py:33
  81.2 12.2 %scatter_fusion = f32[96,4096]{1,0:T(8,128)} fusion(f32[96,4096]{1,0:T(8,128)} %copy.75, s32[96]{0:T(128)S(1)} %fusion.36, f32[96]{0:T(128)} %get-tuple-element.9), kind=kCustom, calls=%fused_computation.10 | custom fusion | flops 96 | bytes 1920 | tf_op jit(solution)/shard_map/scatter-add | solution.py:137
  94.0 60.9 %all-reduce.6.cloned.1.call-done = f32[96,4096]{1,0:T(8,128)} async-done(((f32[96,4096]{1,0:T(8,128)}), f32[96,4096]{1,0:T(8,128)}) %all-reduce.6.cloned.1.call-update) | async-done | bytes 1572880 | tf_op jit(solution)/shard_map/psum | solution.py:140
  154.8 12.7 %fusion.4 = f32[96,512]{1,0:T(8,128)} fusion(f32[96,4096]{1,0:T(8,128)} %all-reduce.6.cloned.1.call-done, f32[1,512,4096]{2,1,0:T(8,128)} %param.19), kind=kOutput, calls=%fused_computation.21 | convolution fusion | flops 2415919104 | bytes 10158080 | tf_op jit(solution)/shard_map/dot_general | solution.py:141
  174.4 17.7 %all-gather.6.cloned.1.call-done = f32[96,4096]{1,0:T(8,128)} async-done(((f32[96,512]{1,0:T(8,128)}), f32[96,4096]{1,0:T(8,128)}) %all-gather.6.cloned.1.call-update) | async-done | bytes 1572880 | tf_op jit(solution)/shard_map/all_gather | solution.py:38
  194.9 5.6 gather_fusion.6
  209.7 3.7 scatter_custom_fusion.2
  215.7 3.8 all-to-all-start
  229.5 3.6 gather_fusion.2
  234.3 4.2 fusion.11
  238.5 11.4 %all-to-all-done = f32[32,17,288]{2,1,0:T(8,128)} async-done(((f32[32,17,288]{2,1,0:T(8,128)}), f32[32,17,288]{2,1,0:T(8,128)}, u32[]{:S(2)}, u32[]{:S(2)}) %all-to-all-start) | async-done | bytes 626720 | tf_op jit(solution)/shard_map/all_to_all | solution.py:121
  256.9 3.9 fusion.38
  262.1 9.4 %scatter_custom_fusion.3 = f32[96,4096]{0,1:T(8,128)S(1)} fusion(s32[1536]{0:T(1024)} %fusion.32, f32[1536,96]{1,0:T(8,128)S(1)} %copy.84, f32[]{:T(128)} %constant.37.clone.1), kind=kCustom, calls=%fused_computation.45 | custom fusion | flops 147456 | bytes 1573376 | tf_op jit(solution)/shard_map/scatter-add | solution.py:33
  273.4 12.3 %scatter_fusion.1 = f32[96,4096]{1,0:T(8,128)} fusion(f32[96,4096]{1,0:T(8,128)} %copy.85, s32[96]{0:T(128)S(1)} %fusion.36, f32[96]{0:T(128)S(1)} %copy-done.45), kind=kCustom, calls=%fused_computation.13 | custom fusion | flops 96 | bytes 1920 | tf_op jit(solution)/shard_map/scatter-add | solution.py:137
  285.9 59.5 %all-reduce.8.cloned.1.call-done = f32[96,4096]{1,0:T(8,128)} async-done(((f32[96,4096]{1,0:T(8,128)}), f32[96,4096]{1,0:T(8,128)}) %all-reduce.8.cloned.1.call-update) | async-done | bytes 1572880 | tf_op jit(solution)/shard_map/psum | solution.py:140
  345.4 12.6 %fusion.2 = f32[96,512]{1,0:T(8,128)} fusion(f32[96,4096]{1,0:T(8,128)} %all-reduce.8.cloned.1.call-done, f32[1,512,4096]{2,1,0:T(8,128)} %param.19), kind=kOutput, calls=%fused_computation.19 | convolution fusion | flops 2415919104 | bytes 10158080 | tf_op jit(solution)/shard_map/dot_general | solution.py:141
  358.9 23.8 %all-gather.8.cloned.1.call-done = f32[96,4096]{1,0:T(8,128)} async-done(((f32[96,512]{1,0:T(8,128)}), f32[96,4096]{1,0:T(8,128)}) %all-gather.8.cloned.1.call-update) | async-done | bytes 1572880 | tf_op jit(solution)/shard_map/all_gather | solution.py:38
  384.6 3.7 gather_fusion.7
  390.6 3.3 scatter_custom_fusion.5
  396.4 3.8 all-to-all-start.1
  407.8 3.6 gather_fusion.4
  412.5 4.8 add_reduce_fusion
  417.4 13.1 %all-to-all-done.1 = f32[32,17,288]{2,1,0:T(8,128)} async-done(((f32[32,17,288]{2,1,0:T(8,128)}), f32[32,17,288]{2,1,0:T(8,128)}, u32[]{:S(2)}, u32[]{:S(2)}) %all-to-all-start.1) | async-done | bytes 626720 | tf_op jit(solution)/shard_map/all_to_all | solution.py:121
  442.1 9.4 %scatter_custom_fusion.6 = f32[96,4096]{0,1:T(8,128)S(1)} fusion(s32[1536]{0:T(1024)} %fusion.32, f32[1536,96]{1,0:T(8,128)S(1)} %copy.94, f32[]{:T(128)} %constant.37.clone.1), kind=kCustom, calls=%fused_computation.43 | custom fusion | flops 147456 | bytes 1573376 | tf_op jit(solution)/shard_map/scatter-add | solution.py:33
  453.3 12.2 %scatter_fusion.2 = f32[96,4096]{1,0:T(8,128)} fusion(f32[96,4096]{1,0:T(8,128)} %copy.95, s32[96]{0:T(128)S(1)} %fusion.36, f32[96]{0:T(128)S(1)} %copy-done.44), kind=kCustom, calls=%fused_computation.16 | custom fusion | flops 96 | bytes 1920 | tf_op jit(solution)/shard_map/scatter-add | solution.py:137
  465.9 59.4 %all-reduce.10.cloned.1.call-done = f32[96,4096]{1,0:T(8,128)} async-done(((f32[96,4096]{1,0:T(8,128)}), f32[96,4096]{1,0:T(8,128)}) %all-reduce.10.cloned.1.call-update) | async-done | bytes 1572880 | tf_op jit(solution)/shard_map/psum | solution.py:140
  525.3 12.7 %fusion = f32[96,512]{1,0:T(8,128)} fusion(f32[96,4096]{1,0:T(8,128)} %all-reduce.10.cloned.1.call-done, f32[1,512,4096]{2,1,0:T(8,128)} %param.19), kind=kOutput, calls=%fused_computation.17 | convolution fusion | flops 2415919104 | bytes 10158080 | tf_op jit(solution)/shard_map/dot_general | solution.py:141
  538.0 24.6 %all-gather.10.cloned.1.call-done = f32[96,4096]{1,0:T(8,128)} async-done(((f32[96,512]{1,0:T(8,128)}), f32[96,4096]{1,0:T(8,128)}) %all-gather.10.cloned.1.call-update) | async-done | bytes 1572880 | tf_op jit(solution)/shard_map/all_gather | solution.py:38
  564.5 3.7 gather_fusion.8
  (207 shorter events, 123.0 us)
Async XLA Ops:
  7.2 18.5 %copy-start.46 = (s32[96]{0:T(128)S(1)}, s32[96]{0:T(128)}, u32[]{:S(2)}) copy-start(s32[96]{0:T(128)} %param.22) | copy-start | bytes 1156
  7.2 23.8 %copy-start.2 = (f32[1,6,3,96,512]{4,3,2,1,0:T(8,128)S(1)}, f32[1,6,3,96,512]{4,3,2,1,0:T(8,128)}, u32[]{:S(2)}) copy-start(f32[1,6,3,96,512]{4,3,2,1,0:T(8,128)} %param.33) | copy-start | bytes 10616836
  7.2 34.3 %all-gather.12.cloned.1.call-start = ((), (), s32[]{:S(2)}) async-start(), calls=%async_computation.8 | async-start | bytes 2359296 | tf_op jit(solution)/shard_map/all_gather | solution.py:38
  9.2 145.7 %all-reduce.6.cloned.1.call-start = ((), (), s32[]{:S(2)}) async-start(), calls=%async_computation.2 | async-start | bytes 3145728 | tf_op jit(solution)/shard_map/psum | solution.py:140
  12.5 11.2 %copy-start.35 = (s32[1536]{0:T(1024)}, s32[1536]{0:T(1024)S(1)}, u32[]{:S(2)}) copy-start(s32[1536]{0:T(1024)S(1)} %reshape_squeeze.5) | copy-start | bytes 18436
  20.2 10.8 %copy-start.25 = (f32[6,3,1,512]{3,1,2,0:T(4,128)S(1)}, f32[6,3,1,512]{3,1,2,0:T(4,128)}, u32[]{:S(2)}) copy-start(f32[6,3,1,512]{3,1,2,0:T(4,128)} %copy.124) | copy-start | bytes 110596
  20.2 10.8 %copy-start.31 = (f32[1,6,512]{2,1,0:T(8,128)S(1)}, f32[1,6,512]{2,1,0:T(8,128)}, u32[]{:S(2)}) copy-start(f32[1,6,512]{2,1,0:T(8,128)} %copy.126) | copy-start | bytes 36868
  23.6 4.2 copy-start.36
  50.7 7.7 %copy-start = (f32[1,6,3,96,512]{4,3,2,1,0:T(8,128)S(1)}, f32[1,6,3,96,512]{4,3,2,1,0:T(8,128)}, u32[]{:S(2)}) copy-start(f32[1,6,3,96,512]{4,3,2,1,0:T(8,128)} %param.34) | copy-start | bytes 10616836
  93.4 98.7 %all-gather.6.cloned.1.call-start = ((), (), s32[]{:S(2)}) async-start(), calls=%async_computation.3 | async-start | bytes 1769472 | tf_op jit(solution)/shard_map/all_gather | solution.py:38
  215.7 34.1 %all-to-all-start = ((f32[32,17,288]{2,1,0:T(8,128)}), f32[32,17,288]{2,1,0:T(8,128)}, u32[]{:S(2)}, u32[]{:S(2)}) async-start(f32[32,17,288]{2,1,0:T(8,128)} %all_to_all.16), calls=%async_computation | async-start | bytes 2359296 | tf_op jit(solution)/shard_map/all_to_all | solution.py:121
  219.6 125.8 %all-reduce.8.cloned.1.call-start = ((), (), s32[]{:S(2)}) async-start(), calls=%async_computation.4 | async-start | bytes 3145728 | tf_op jit(solution)/shard_map/psum | solution.py:140
  256.8 4.8 copy-start.14
  260.8 10.7 %copy-start.41 = (f32[1,1,512]{2,1,0:T(1,128)S(1)}, f32[1,1,512]{2,1,0:T(1,128)}, u32[]{:S(2)}) copy-start(f32[1,1,512]{2,1,0:T(1,128)} %get-tuple-element.45) | copy-start | bytes 6148
  261.8 11.6 %copy-start.45 = (f32[96]{0:T(128)S(1)}, f32[96]{0:T(128)}, u32[]{:S(2)}) copy-start(f32[96]{0:T(128)} %multiply_select_fusion.1) | copy-start | bytes 1156
  285.6 72.4 %copy-start.18 = (f32[3,96,512]{2,1,0:T(8,128)S(1)}, f32[3,96,512]{2,1,0:T(8,128)}, u32[]{:S(2)}) copy-start(f32[3,96,512]{2,1,0:T(8,128)} %get-tuple-element.3) | copy-start | bytes 1769476
  285.7 97.0 %all-gather.8.cloned.1.call-start = ((), (), s32[]{:S(2)}) async-start(), calls=%async_computation.5 | async-start | bytes 1769472 | tf_op jit(solution)/shard_map/all_gather | solution.py:38
  358.0 26.5 %copy-start.33 = (s32[2048]{0:T(1024)S(1)}, s32[2048]{0:T(1024)}, u32[]{:S(2)}) copy-start(s32[2048]{0:T(1024)} %pad_clamp_fusion) | copy-start | bytes 24580
  384.5 5.4 copy-start.11
  384.5 5.4 copy-start.15
  384.5 5.4 copy-start.38
  393.9 18.6 %copy-start.1 = (f32[1,6,3,96,512]{4,3,2,1,0:T(8,128)S(1)}, f32[1,6,3,96,512]{4,3,2,1,0:T(8,128)}, u32[]{:S(2)}) copy-start(f32[1,6,3,96,512]{4,3,2,1,0:T(8,128)} %param.34) | copy-start | bytes 10616836
  396.4 34.1 %all-to-all-start.1 = ((f32[32,17,288]{2,1,0:T(8,128)}), f32[32,17,288]{2,1,0:T(8,128)}, u32[]{:S(2)}, u32[]{:S(2)}) async-start(f32[32,17,288]{2,1,0:T(8,128)} %all_to_all.19), calls=%async_computation.1 | async-start | bytes 2359296 | tf_op jit(solution)/shard_map/all_to_all | solution.py:121
  400.2 125.1 %all-reduce.10.cloned.1.call-start = ((), (), s32[]{:S(2)}) async-start(), calls=%async_computation.6 | async-start | bytes 3145728 | tf_op jit(solution)/shard_map/psum | solution.py:140
  431.9 4.8 copy-start.42
  440.9 10.5 %copy-start.40 = (f32[1,1,512]{2,1,0:T(1,128)S(1)}, f32[1,1,512]{2,1,0:T(1,128)}, u32[]{:S(2)}) copy-start(f32[1,1,512]{2,1,0:T(1,128)} %get-tuple-element.43) | copy-start | bytes 6148
  441.8 11.5 %copy-start.44 = (f32[96]{0:T(128)S(1)}, f32[96]{0:T(128)}, u32[]{:S(2)}) copy-start(f32[96]{0:T(128)} %multiply_select_fusion) | copy-start | bytes 1156
  465.5 97.0 %all-gather.10.cloned.1.call-start = ((), (), s32[]{:S(2)}) async-start(), calls=%async_computation.7 | async-start | bytes 1769472 | tf_op jit(solution)/shard_map/all_gather | solution.py:38
  538.0 26.5 %copy-start.34 = (s32[2048]{0:T(1024)S(1)}, s32[2048]{0:T(1024)}, u32[]{:S(2)}) copy-start(s32[2048]{0:T(1024)} %pad_clamp_fusion) | copy-start | bytes 24580
  564.4 5.4 copy-start.8
  564.4 5.4 copy-start.17
  564.5 5.4 copy-start.39
  (25 other events, 47.3 us)
Sparse Core Ops, SparseCore 0:
  9.6 31.8 all-gather.11
  93.5 61.2 all-reduce.5
  167.6 24.4 all-gather.5
  285.8 59.5 all-reduce.7
  358.2 24.4 all-gather.7
  465.7 59.5 all-reduce.9
  538.1 24.4 all-gather.9
where the time goes:
time: 588 us; the launch traced here: 578 us
  waiting for transfers between devices  279 us (47%)
  other arithmetic  122 us (21%)
  local copies, waits for them, and re-layouts  115 us (20%)
  matrix products  38 us (6%)
  between operations  15.4 us (3%)
  starting transfers between devices  9.43 us (2%)
    psum x3, waiting for transfers between devices, on_device(): summed = lax.psum(injection, 'line')  180 us
    all_gather x4, waiting for transfers between devices, gather_full(): return lax.all_gather(block, 'line', axis=1, tiled=True)  74.8 us
    dot_general x3, matrix products, on_device(): lax.dot_general(summed, inverse_block, (((1,), (1,)), ((), ())), precisio...  38 us
    scatter-add x3, other arithmetic, on_device(): injection.at[scenario_range, fault_local]  36.7 us
    scatter-add x3, other arithmetic, spread_ends(): return jnp.zeros((history.shape[1], node_count), jnp.float32).at[:, termi...  29.3 us
    all_to_all x2, waiting for transfers between devices, on_device(): lax.all_to_all(buffer, ('net', 'line'), split_axis=0, concat_axis=0, tile...  24.5 us
    reduce_sum x6, other arithmetic, on_device(): history = (jnp.sum(wave_now, axis=0) - jnp.sum(admits, axis=0)) * live_float  20.3 us
    gather x4, local copies, waits for them, and re-layouts, terminal_values(): picked = jnp.take(voltage, terminal.reshape(-1), axis=1)  18.5 us
  transfers between devices with their start and end apart: 9, of which 9 were waited for; matrix products, arithmetic and copies ran while one was open for 11% of the time, Pallas kernels for 0%

commit v1 on v0

v1 whole, which is shorter than its diff:
```python
import functools

import jax
import jax.numpy as jnp
from jax import lax
from jax.experimental import pallas as pl
from jax.experimental.pallas import tpu as pltpu
from jax.sharding import PartitionSpec as P

STEPS = 3
CORES = 2
MESH = pl.DeviceIdType.MESH


def mix_residue(residue, vector):
    return (
        residue[:, :, 0, None, :] * vector[0]
        + residue[:, :, 1, None, :] * vector[1]
        + residue[:, :, 2, None, :] * vector[2]
    )


def select_delayed(buffer, delay_local):
    depth_count = buffer.shape[0]
    chosen = delay_local[None, :] == jnp.arange(1, depth_count + 1, dtype=jnp.int32)[:, None]
    return jnp.sum(jnp.where(chosen[:, None, None, :], buffer, 0.0), axis=0)


def split_two(value):
    high = value.astype(jnp.bfloat16)
    low = (value - high.astype(jnp.float32)).astype(jnp.bfloat16)
    return high, low


def dot_nt(left, right):
    return lax.dot_general(left, right, (((1,), (1,)), ((), ())), preferred_element_type=jnp.float32)


def dot_nn(left, right):
    return lax.dot_general(left, right, (((1,), (0,)), ((), ())), preferred_element_type=jnp.float32)


def positions(chips):
    line = lax.axis_index("line")
    return line, line // CORES, line % CORES


def greet(chips):
    line, z, core = positions(chips)
    barrier = pltpu.get_barrier_semaphore()
    pl.semaphore_signal(barrier, inc=1, device_id={"line": z * CORES + 1 - core}, device_id_type=MESH)
    for i in range(chips - 1):
        peer = lax.rem(z + 1 + i, chips) * CORES + core
        pl.semaphore_signal(barrier, inc=1, device_id={"line": peer}, device_id_type=MESH)
    pl.semaphore_wait(barrier, chips)


def remote(src, dst, send, recv, line_index):
    return pltpu.make_async_remote_copy(
        src_ref=src, dst_ref=dst, send_sem=send, recv_sem=recv,
        device_id={"line": line_index}, device_id_type=MESH,
    )


def gather_blocks(chips, buf, sems, consume):
    c_send, c_recv, d_send, d_recv = sems
    line, z, core = positions(chips)
    partner = z * CORES + 1 - core

    def across(i):
        peer = lax.rem(z + 1 + i, chips) * CORES + core
        return remote(buf.at[line], buf.at[line], c_send.at[i], c_recv.at[i], peer)

    def over(i, block):
        return remote(buf.at[block], buf.at[block], d_send.at[i], d_recv.at[i], partner)

    for i in range(chips - 1):
        across(i).start()

    def step(k, carry):
        i = lax.rem(k + chips - 1, chips)
        source = lax.rem(z + 2 * chips - 1 - i, chips)
        block = source * CORES + core

        @pl.when(k > 0)
        def _():
            remote(buf.at[block], buf.at[block], c_send.at[i], c_recv.at[i], partner).wait_recv()

        over(i, block).start()
        consume(block)
        other = source * CORES + 1 - core
        remote(buf.at[other], buf.at[other], d_send.at[i], d_recv.at[i], partner).wait_recv()
        consume(other)
        return carry

    lax.fori_loop(0, chips, step, 0)
    for i in range(chips - 1):
        across(i).wait_send()
    for i in range(chips):
        source = lax.rem(z + 2 * chips - 1 - i, chips)
        over(i, source * CORES + core).wait_send()


def one_hot(term_ref, phase, block, width):
    slots = term_ref.shape[1]
    rows = lax.broadcasted_iota(jnp.int32, (width, slots), 0) + block * width
    return (rows == term_ref[phase : phase + 1, :]).astype(jnp.float32).astype(jnp.bfloat16)


def pick_terminals(chips, buf, sems, term_ref, ends_ref):
    phases, count, _ = ends_ref.shape
    width = buf.shape[2]
    ends_ref[...] = jnp.zeros_like(ends_ref)

    def consume(block):
        both = jnp.concatenate(split_two(buf[block]), axis=0)
        for p in range(phases):
            got = dot_nn(both, one_hot(term_ref, p, block, width))
            ends_ref[p] += got[:count] + got[count:]

    gather_blocks(chips, buf, sems, consume)


def prior_kernel(chips, prior_ref, term_ref, ends_ref, vfull, *sems):
    line, z, core = positions(chips)
    greet(chips)
    vfull[line] = prior_ref[...]
    pick_terminals(chips, vfull, sems, term_ref, ends_ref)


def step_kernel(
    chips, h_ref, term_ref, add_ref, inv_hbm, volt_ref, ends_ref,
    part, r1, summed, r2, ifull, vfull, inv, inv_sem,
    a_send, a_recv, b_send, b_recv, *sems,
):
    line, z, core = positions(chips)
    partner = z * CORES + 1 - core
    phases = h_ref.shape[0]
    count, width = add_ref.shape
    load = pltpu.make_async_copy(inv_hbm, inv, inv_sem)
    load.start()
    greet(chips)

    def scatter_block(block):
        total = jnp.zeros((count, width), jnp.float32)
        for p in range(phases):
            both = jnp.concatenate(split_two(h_ref[p]), axis=0)
            got = dot_nt(both, one_hot(term_ref, p, block, width))
            total = total + (got[:count] + got[count:])
        return total

    def swap(i):
        return remote(part.at[i], r1.at[i], a_send.at[i], a_recv.at[i], partner)

    def pass_on(i):
        peer = lax.rem(z + 1 + i, chips) * CORES + core
        return remote(summed.at[i], r2.at[i], b_send.at[i], b_recv.at[i], peer)

    def scatter_step(i, carry):
        target = lax.rem(z + 1 + i, chips)
        part[i] = scatter_block(target * CORES + 1 - core)
        swap(i).start()
        own = scatter_block(target * CORES + core)
        swap(i).wait_recv()
        summed[i] = own + r1[i]

        @pl.when(i < chips - 1)
        def _():
            pass_on(i).start()

        return carry

    lax.fori_loop(0, chips, scatter_step, 0)
    total = summed[chips - 1] + add_ref[...]
    for i in range(chips - 1):
        pass_on(i).wait_recv()
        total = total + r2[i]
    ifull[line] = total
    load.wait()
    volt_ref[...] = jnp.zeros_like(volt_ref)

    def solve(block):
        both = jnp.concatenate(split_two(ifull[block]), axis=0)
        start = pl.multiple_of(block * width, width)
        high, low = split_two(inv[:, pl.ds(start, width)])
        got = dot_nt(both, high)
        volt_ref[...] += got[:count] + (got[count:] + dot_nt(both[:count], low))

    gather_blocks(chips, ifull, sems[:4], solve)
    vfull[line] = volt_ref[...]
    pick_terminals(chips, vfull, sems[4:], term_ref, ends_ref)
    for i in range(chips):
        swap(i).wait_send()
    for i in range(chips - 1):
        pass_on(i).wait_send()


def gather_sems(chips):
    return [
        pltpu.SemaphoreType.DMA((chips,)),
        pltpu.SemaphoreType.DMA((chips,)),
        pltpu.SemaphoreType.DMA((chips,)),
        pltpu.SemaphoreType.DMA((chips,)),
    ]


def vmem():
    return pl.BlockSpec(memory_space=pltpu.VMEM)


def prior_ends(prior, terminal, lines):
    chips = lines // CORES
    count, width = prior.shape
    return pl.pallas_call(
        functools.partial(prior_kernel, chips),
        out_shape=jax.ShapeDtypeStruct((terminal.shape[0], count, terminal.shape[1]), jnp.float32),
        in_specs=[vmem(), vmem()],
        out_specs=vmem(),
        scratch_shapes=[pltpu.VMEM((lines, count, width), jnp.float32)] + gather_sems(chips),
        compiler_params=pltpu.CompilerParams(collective_id=1, has_side_effects=True),
        name="prior_ends",
    )(prior, terminal)


def network_step(h, terminal, extra, inverse, lines):
    chips = lines // CORES
    count, width = extra.shape
    block = lambda n: pltpu.VMEM((n, count, width), jnp.float32)
    return pl.pallas_call(
        functools.partial(step_kernel, chips),
        out_shape=(
            jax.ShapeDtypeStruct((count, width), jnp.float32),
            jax.ShapeDtypeStruct(h.shape, jnp.float32),
        ),
        in_specs=[vmem(), vmem(), vmem(), pl.BlockSpec(memory_space=pltpu.HBM)],
        out_specs=(vmem(), vmem()),
        scratch_shapes=[
            block(chips), block(chips), block(chips), block(chips), block(lines), block(lines),
            pltpu.VMEM(inverse.shape, jnp.float32),
            pltpu.SemaphoreType.DMA(()),
        ] + gather_sems(chips) + gather_sems(chips) + gather_sems(chips),
        compiler_params=pltpu.CompilerParams(
            collective_id=0, has_side_effects=True, vmem_limit_bytes=40 * 2**20
        ),
        name="network_step",
    )(h, terminal, extra, inverse)


def on_device(
    conductance_inverse,
    prior_voltage,
    sources,
    fault_node,
    fault_conductance,
    terminal_node,
    ownership,
    partner,
    delay_steps,
    surge_conductance,
    pole_wave,
    residue_wave,
    pole_admit,
    residue_admit,
    wave_state,
    admit_state,
    wave_history,
):
    inverse_block = conductance_inverse[0]
    row_count = inverse_block.shape[0]
    node_count = inverse_block.shape[1]
    line_index = lax.axis_index("line")
    net_index = lax.axis_index("net")
    line_count = lax.axis_size("line")
    devices = lax.axis_size("net") * line_count
    slot_count = ownership.shape[1]
    capacity = (slot_count + devices - 2) // (devices - 1)
    is_live = ownership[0] > 0
    live_float = is_live.astype(jnp.float32)
    terminal = terminal_node[0]
    delay_local = delay_steps[0]
    surge_local = surge_conductance[0]
    partners = partner[0]
    slot_range = jnp.arange(slot_count, dtype=jnp.int32)
    earlier = (
        (partners[:, None] == partners[None, :])
        & is_live[:, None]
        & (slot_range[:, None] < slot_range[None, :])
    )
    slot_rank = jnp.sum(earlier.astype(jnp.int32), axis=0)
    position = jnp.where(is_live, partners * capacity + slot_rank, devices * capacity)
    place = jnp.arange(devices * capacity, dtype=jnp.int32)
    packer = (place[:, None] == position[None, :]).astype(jnp.float32)
    fault_local = fault_node - (net_index * node_count + line_index * row_count)
    fault_hit = fault_local[:, None] == jnp.arange(row_count, dtype=jnp.int32)[None, :]
    fault_weight = jnp.where(fault_hit, fault_conductance[:, None], 0.0)
    wave_decay = pole_wave[0][:, None, None, :]
    admit_decay = pole_admit[0][:, None, None, :]
    wave_res = residue_wave[0]
    admit_res = residue_admit[0]
    voltage_rows = prior_voltage[0]
    wave_now = wave_state[0]
    admits = admit_state[0]
    history_buffer = wave_history[0]
    ends = prior_ends(voltage_rows, terminal, line_count)
    outgoing = None
    current = None
    for step_index in range(STEPS):
        if step_index == 0:
            wave_now = wave_decay * wave_now + mix_residue(
                wave_res, select_delayed(history_buffer, delay_local)
            )
            admits = admit_decay * admits + mix_residue(admit_res, ends)
        else:
            rows = outgoing.reshape(-1, slot_count)
            buffer = lax.dot_general(
                packer, rows, (((1,), (1,)), ((), ())), precision=lax.Precision.HIGHEST
            )
            arrived = lax.all_to_all(
                buffer, ("net", "line"), split_axis=0, concat_axis=0, tiled=True
            )
            admits = admit_decay * admits + mix_residue(admit_res, ends)
            arrived = lax.dot_general(
                arrived, packer, (((0,), (0,)), ((), ())), precision=lax.Precision.HIGHEST
            ).reshape(outgoing.shape)
            history_buffer = jnp.concatenate([arrived[None], history_buffer[:-1]], axis=0)
            wave_now = wave_decay * wave_now + mix_residue(
                wave_res, select_delayed(history_buffer, delay_local)
            )
        history = (jnp.sum(wave_now, axis=0) - jnp.sum(admits, axis=0)) * live_float
        extra = sources[step_index, 0][None, :] - fault_weight * voltage_rows
        voltage_rows, ends = network_step(history, terminal, extra, inverse_block, line_count)
        if step_index + 1 < STEPS:
            outgoing = (2.0 * surge_local * ends - history) * live_float
        else:
            current = (surge_local * ends - history) * live_float
    return (voltage_rows[None], current[None])


def solution(mesh):
    return jax.shard_map(
        on_device,
        mesh=mesh,
        in_specs=(
            P("net", "line", None),
            P("net", None, "line"),
            P(None, "net", "line"),
            P(),
            P(),
            P("net", None, "line"),
            P("net", "line"),
            P("net", "line"),
            P("net", "line"),
            P("net", "line"),
            P("net", None, "line"),
            P("net", None, None, None, "line"),
            P("net", None, "line"),
            P("net", None, None, None, "line"),
            P("net", None, None, None, "line"),
            P("net", None, None, None, "line"),
            P("net", None, None, None, "line"),
        ),
        out_specs=(P("net", None, "line"), P("net", None, None, "line")),
        check_vma=False,
    )
```

time: 588 us -> 334 us (0.57); the launches traced: 578 us -> 333 us
  waiting for transfers between devices: 279 us -> 48.6 us
  Pallas kernels: 0 us -> 215 us
  other arithmetic: 122 us -> 26.6 us
  local copies, waits for them, and re-layouts: 115 us -> 20 us
  matrix products: 38 us -> 8.42 us
  between operations: 15.4 us -> 1.96 us
    pallas_call x0 -> x4, Pallas kernels: none -> 215 us  [the longest x3 190 us: network_step(): pl.pallas_call(functools.partial(step_kernel, chips), out_shape=(jax.Shap...]
    psum x3 -> x0, waiting for transfers between devices: 180 us -> none  [on_device(): summed = lax.psum(injection, 'line')]
    all_gather x4 -> x0, waiting for transfers between devices: 74.8 us -> none  [gather_full(): return lax.all_gather(block, 'line', axis=1, tiled=True)]
    scatter-add x6 -> x0, other arithmetic: 66 us -> none  [the longest x3 36.7 us: on_device(): injection.at[scenario_range, fault_local]]
    gather x11 -> x0, local copies, waits for them, and re-layouts: 36 us -> none  [the longest x4 18.5 us: terminal_values(): picked = jnp.take(voltage, terminal.reshape(-1), axis=1)]
    dot_general x3 -> x4, matrix products: 38 us -> 8.42 us  [the longest x2 5.06 us: on_device(): lax.dot_general(packer, rows, (((1,), (1,)), ((), ())), precision=lax.Pre...]
    all_to_all x2, waiting for transfers between devices: 24.5 us -> 48.6 us  [on_device(): lax.all_to_all(buffer, ('net', 'line'), split_axis=0, concat_axis=0, tile...]
    select_n x13 -> x1, other arithmetic: 16.5 us -> 0.01 us  [on_device(): jnp.where(is_live, partners * capacity + slot_rank, devices * capacity)]
  transfers between devices with their start and end apart: 9 -> 2, of which waited for: 9 -> 2; matrix products, arithmetic and copies ran while one was open for 11% -> 3% of each run, Pallas kernels for 0% -> 0%
where the time goes in v1:
time: 334 us; the launch traced here: 333 us
  Pallas kernels  215 us (64%)
  waiting for transfers between devices  48.6 us (15%)
  other arithmetic  26.6 us (8%)
  local copies, waits for them, and re-layouts  20 us (6%)
  starting transfers between devices  12.7 us (4%)
  matrix products  8.42 us (3%)
    pallas_call x3, Pallas kernels, network_step(): pl.pallas_call(functools.partial(step_kernel, chips), out_shape=(jax.Shap...  190 us
    all_to_all x2, waiting for transfers between devices, on_device(): lax.all_to_all(buffer, ('net', 'line'), split_axis=0, concat_axis=0, tile...  48.6 us
    pallas_call x1, Pallas kernels, prior_ends(): pl.pallas_call(functools.partial(prior_kernel, chips), out_shape=jax.Shap...  24.5 us
    reduce_sum x6, other arithmetic, on_device(): history = (jnp.sum(wave_now, axis=0) - jnp.sum(admits, axis=0)) * live_float  18.6 us
    all_to_all x2, starting transfers between devices, on_device(): lax.all_to_all(buffer, ('net', 'line'), split_axis=0, concat_axis=0, tile...  12.7 us
    unnamed x162, local copies, waits for them, and re-layouts  10.8 us
  transfers between devices with their start and end apart: 2, of which 2 were waited for; matrix products, arithmetic and copies ran while one was open for 3% of the time, Pallas kernels for 0%

profile of v1, /device:TPU:0, one launch (start us, length us, event | category | flops | bytes accessed | tf_op | source)
XLA Modules:
  0.0 333.2 jit_solution(16209524137777095615)
XLA Ops:
  0.7 0.8 broadcast_compare_fusion.1
  1.6 2.1 fusion.5
  4.5 24.5 %prior_ends.1 = f32[3,96,512]{2,1,0:T(8,128)} custom-call(f32[96,512]{1,0:T(8,128)} %bitcast.147, s32[3,512]{1,0:T(4,128)} %bitcast.132), custom_call_target="tpu_custom_call" | custom-call | tf_op jit(solution)/shard_map/prior_ends/pallas_call | solution.py:214
  29.1 1.2 slice_bitcast_fusion.18
  31.5 3.1 fusion.22
  34.7 3.2 fusion.23
  38.3 3.4 %copy-done = f32[1,512,4096]{2,1,0:T(8,128)S(1)} copy-done((f32[1,512,4096]{2,1,0:T(8,128)S(1)}, f32[1,512,4096]{2,1,0:T(8,128)}, u32[]{:S(2)}) %copy-start) | copy-done | bytes 8388632
  41.7 65.1 %network_step.3 = (f32[96,512]{1,0:T(8,128)S(1)}, f32[3,96,512]{2,1,0:T(8,128)S(1)}) custom-call(f32[3,96,512]{2,1,0:T(8,128)S(1)} %subtract_multiply_fusion.4.h_ref, s32[3,512]{1,0:T(4,128)S(1)} %bitcast.133, f32[96,512]{1,0:T(8,128)S(1)} %fusion.19.add_ref, f32[512,4096]{1,0:T(8,128)S(1)} %bitcast.127), custom_call_target="tpu_custom_call" | custom-call | tf_op jit(solution)/shard_map/network_step/pallas_call | solution.py:229
  107.2 2.6 fusion.11
  109.8 7.1 %all-to-all-start = ((f32[32,17,288]{2,1,0:T(8,128)}), f32[32,17,288]{2,1,0:T(8,128)S(1)}, u32[]{:S(2)}, u32[]{:S(2)}) async-start(f32[32,17,288]{2,1,0:T(8,128)} %fusion.11), calls=%async_computation | async-start | bytes 2359296 | tf_op jit(solution)/shard_map/all_to_all | solution.py:318
  117.2 2.1 slice_bitcast_fusion
  119.8 2.6 fusion.7
  122.4 24.6 %all-to-all-done = f32[32,17,288]{2,1,0:T(8,128)S(1)} async-done(((f32[32,17,288]{2,1,0:T(8,128)}), f32[32,17,288]{2,1,0:T(8,128)S(1)}, u32[]{:S(2)}, u32[]{:S(2)}) %all-to-all-start) | async-done | bytes 626720 | tf_op jit(solution)/shard_map/all_to_all | solution.py:318
  147.0 1.0 all_to_all.13
  148.1 1.4 copy.28
  149.5 1.6 convolution_bitcast_fusion.1
  151.2 1.5 fusion.8
  153.8 1.8 fusion.6
  155.8 1.2 slice-done.1
  157.0 62.6 %network_step.4 = (f32[96,512]{1,0:T(8,128)S(1)}, f32[3,96,512]{2,1,0:T(8,128)S(1)}) custom-call(f32[3,96,512]{2,1,0:T(8,128)S(1)} %subtract_multiply_fusion.2.h_ref, s32[3,512]{1,0:T(4,128)S(1)} %bitcast.134, f32[96,512]{1,0:T(8,128)S(1)} %fusion.20.add_ref, f32[512,4096]{1,0:T(8,128)S(1)} %bitcast.130), custom_call_target="tpu_custom_call" | custom-call | tf_op jit(solution)/shard_map/network_step/pallas_call | solution.py:229
  219.8 2.5 fusion.9
  222.3 5.6 %all-to-all-start.1 = ((f32[32,17,288]{2,1,0:T(8,128)}), f32[32,17,288]{2,1,0:T(8,128)S(1)}, u32[]{:S(2)}, u32[]{:S(2)}) async-start(f32[32,17,288]{2,1,0:T(8,128)} %fusion.9), calls=%async_computation.1 | async-start | bytes 2359296 | tf_op jit(solution)/shard_map/all_to_all | solution.py:318
  227.9 0.8 fusion.21.add_ref
  228.8 5.1 %add_reduce_fusion = f32[3,96,512]{2,1,0:T(8,128)} fusion(f32[96,512]{1,0:T(8,128)S(1)} %get-tuple-element.15, f32[96,512]{1,0:T(8,128)S(1)} %get-tuple-element.16, f32[96,512]{1,0:T(8,128)S(1)} %get-tuple-element.14, f32[96,512]{1,0:T(8,128)S(1)} %copy-done.30, f32[96,512]{1,0:T(8,128)} %copy-done.31, f32[96,512]{1,0:T(8,128)S(1)} %copy-done.28, ...), kind=kLoop, calls=%fused_computation.4 | loop fusion | flops 19316736 | bytes 6021120 | tf_op jit(solution)/shard_map/reduce_sum | solution.py:329
  233.9 24.0 %all-to-all-done.1 = f32[32,17,288]{2,1,0:T(8,128)S(1)} async-done(((f32[32,17,288]{2,1,0:T(8,128)}), f32[32,17,288]{2,1,0:T(8,128)S(1)}, u32[]{:S(2)}, u32[]{:S(2)}) %all-to-all-start.1) | async-done | bytes 626720 | tf_op jit(solution)/shard_map/all_to_all | solution.py:318
  257.9 1.0 all_to_all.15
  258.9 1.5 copy.30
  260.5 1.7 convolution_bitcast_fusion
  262.7 2.7 add_reduce_fusion.1
  265.6 3.4 %copy-done.1 = f32[1,512,4096]{2,1,0:T(8,128)S(1)} copy-done((f32[1,512,4096]{2,1,0:T(8,128)S(1)}, f32[1,512,4096]{2,1,0:T(8,128)}, u32[]{:S(2)}) %copy-start.1) | copy-done | bytes 8388632
  269.0 62.6 %network_step.5 = (f32[96,512]{1,0:T(8,128)S(1)}, f32[3,96,512]{2,1,0:T(8,128)S(1)}) custom-call(f32[3,96,512]{2,1,0:T(8,128)S(1)} %subtract_multiply_fusion.h_ref, s32[3,512]{1,0:T(4,128)S(1)} %bitcast.135, f32[96,512]{1,0:T(8,128)S(1)} %fusion.21.add_ref, f32[512,4096]{1,0:T(8,128)S(1)} %bitcast.131), custom_call_target="tpu_custom_call" | custom-call | tf_op jit(solution)/shard_map/network_step/pallas_call | solution.py:229
  331.6 0.9 multiply_bitcast_fusion
  (186 shorter events, 5.8 us)
Async XLA Ops:
  0.7 29.6 %copy-start.56 = (f32[1,6,3,3,512]{4,0,3,2,1:T(1,128)S(1)}, f32[1,6,3,3,512]{4,0,3,2,1:T(1,128)}, u32[]{:S(2)}) copy-start(f32[1,6,3,3,512]{4,0,3,2,1:T(1,128)} %param.30) | copy-start | bytes 331780
  1.5 28.9 %copy-start.62 = (f32[1,6,512]{2,0,1:T(1,128)S(1)}, f32[1,6,512]{2,0,1:T(1,128)}, u32[]{:S(2)}) copy-start(f32[1,6,512]{2,0,1:T(1,128)} %param.29) | copy-start | bytes 36868
  1.5 28.9 %copy-start.66 = (s32[1,512]{1,0:T(1,128)S(1)}, s32[1,512]{1,0:T(1,128)}, u32[]{:S(2)}) copy-start(s32[1,512]{1,0:T(1,128)} %param.23) | copy-start | bytes 6148
  1.5 29.0 %copy-start.68 = (f32[3,1,512]{2,1,0:T(1,128)S(1)}, f32[3,1,512]{2,1,0:T(1,128)}, u32[]{:S(2)}) copy-start(f32[3,1,512]{2,1,0:T(1,128)} %param.19) | copy-start | bytes 18436
  1.5 29.6 %copy-start.63 = (f32[1,512]{1,0:T(1,128)S(1)}, f32[1,512]{1,0:T(1,128)}, u32[]{:S(2)}) copy-start(f32[1,512]{1,0:T(1,128)} %param.26) | copy-start | bytes 6148
  1.5 29.6 %copy-start.60 = (s32[1,512]{1,0:T(1,128)S(1)}, s32[1,512]{1,0:T(1,128)}, u32[]{:S(2)}) copy-start(s32[1,512]{1,0:T(1,128)} %param.24) | copy-start | bytes 6148
  1.6 29.9 %copy-start.73 = (s32[96]{0:T(128)S(1)}, s32[96]{0:T(128)}, u32[]{:S(2)}) copy-start(s32[96]{0:T(128)} %param.20) | copy-start | bytes 1156
  3.7 27.8 %copy-start.7 = (f32[96,512]{1,0:T(8,128)}, f32[96,512]{1,0:T(8,128)S(1)}, u32[]{:S(2)}) copy-start(f32[96,512]{1,0:T(8,128)S(1)} %get-tuple-element.31) | copy-start | bytes 589828
  3.9 30.8 %copy-start.32 = (f32[6,3,1,512]{3,1,2,0:T(4,128)}, f32[6,3,1,512]{3,1,2,0:T(4,128)S(1)}, u32[]{:S(2)}) copy-start(f32[6,3,1,512]{3,1,2,0:T(4,128)S(1)} %copy.63) | copy-start | bytes 110596
  3.9 30.8 %copy-start.50 = (f32[1,6,512]{2,1,0:T(8,128)}, f32[1,6,512]{2,1,0:T(8,128)S(1)}, u32[]{:S(2)}) copy-start(f32[1,6,512]{2,1,0:T(8,128)S(1)} %copy.65) | copy-start | bytes 36868
  30.2 7.7 %copy-start.10 = (f32[96,512]{1,0:T(8,128)}, f32[96,512]{1,0:T(8,128)S(1)}, u32[]{:S(2)}) copy-start(f32[96,512]{1,0:T(8,128)S(1)} %get-tuple-element.26) | copy-start | bytes 589828
  30.2 7.7 %copy-start.13 = (f32[96,512]{1,0:T(8,128)}, f32[96,512]{1,0:T(8,128)S(1)}, u32[]{:S(2)}) copy-start(f32[96,512]{1,0:T(8,128)S(1)} %get-tuple-element.27) | copy-start | bytes 589828
  30.2 7.7 %copy-start.16 = (f32[96,512]{1,0:T(8,128)}, f32[96,512]{1,0:T(8,128)S(1)}, u32[]{:S(2)}) copy-start(f32[96,512]{1,0:T(8,128)S(1)} %get-tuple-element.28) | copy-start | bytes 589828
  30.4 7.5 %copy-start.41 = (f32[6,3,1,512]{3,1,2,0:T(4,128)}, f32[6,3,1,512]{3,1,2,0:T(4,128)S(1)}, u32[]{:S(2)}) copy-start(f32[6,3,1,512]{3,1,2,0:T(4,128)S(1)} %copy.62) | copy-start | bytes 110596
  30.4 7.5 %copy-start.53 = (f32[1,6,512]{2,1,0:T(8,128)}, f32[1,6,512]{2,1,0:T(8,128)S(1)}, u32[]{:S(2)}) copy-start(f32[1,6,512]{2,1,0:T(8,128)S(1)} %copy.64) | copy-start | bytes 36868
  31.1 75.7 %copy-start.58 = (f32[512]{0:T(512)}, f32[512]{0:T(512)S(1)}, u32[]{:S(2)}) copy-start(f32[512]{0:T(512)S(1)} %broadcast_multiply_fusion) | copy-start | bytes 6148
  31.4 75.6 %copy-start.57 = (s32[1,512]{1,0:T(1,128)}, s32[1,512]{1,0:T(1,128)S(1)}, u32[]{:S(2)}) copy-start(s32[1,512]{1,0:T(1,128)S(1)} %compare_select_fusion) | copy-start | bytes 6148
  106.8 10.2 %copy-start.65 = (f32[1,1,512]{2,1,0:T(1,128)S(1)}, f32[1,1,512]{2,1,0:T(1,128)}, u32[]{:S(2)}) copy-start(f32[1,1,512]{2,1,0:T(1,128)} %get-tuple-element.40) | copy-start | bytes 6148
  106.8 10.2 %copy-start.70 = (f32[96]{0:T(128)S(1)}, f32[96]{0:T(128)}, u32[]{:S(2)}) copy-start(f32[96]{0:T(128)} %param.21) | copy-start | bytes 1156
  106.8 10.2 %copy-start.72 = (s32[96]{0:T(128)S(1)}, s32[96]{0:T(128)}, u32[]{:S(2)}) copy-start(s32[96]{0:T(128)} %copy-done.71) | copy-start | bytes 1156
  107.2 10.0 %copy-start.48 = (pred[32,17,512]{2,0,1:T(32,128)(4,1)}, pred[32,17,512]{2,0,1:T(32,128)(4,1)S(1)}, u32[]{:S(2)}) copy-start(pred[32,17,512]{2,0,1:T(32,128)(4,1)S(1)} %broadcast_compare_fusion) | copy-start | bytes 835588
  109.8 37.3 %all-to-all-start = ((f32[32,17,288]{2,1,0:T(8,128)}), f32[32,17,288]{2,1,0:T(8,128)S(1)}, u32[]{:S(2)}, u32[]{:S(2)}) async-start(f32[32,17,288]{2,1,0:T(8,128)} %fusion.11), calls=%async_computation | async-start | bytes 2359296 | tf_op jit(solution)/shard_map/all_to_all | solution.py:318
  156.9 62.6 %copy-start.59 = (f32[512]{0:T(512)S(1)}, f32[512]{0:T(512)}, u32[]{:S(2)}) copy-start(f32[512]{0:T(512)} %copy-done.58) | copy-start | bytes 6148
  156.9 62.8 %copy-start.49 = (pred[32,17,512]{2,0,1:T(32,128)(4,1)S(1)}, pred[32,17,512]{2,0,1:T(32,128)(4,1)}, u32[]{:S(2)}) copy-start(pred[32,17,512]{2,0,1:T(32,128)(4,1)} %copy-done.48) | copy-start | bytes 835588
  219.7 9.0 %copy-start.12 = (f32[96,512]{1,0:T(8,128)S(1)}, f32[96,512]{1,0:T(8,128)}, u32[]{:S(2)}) copy-start(f32[96,512]{1,0:T(8,128)} %copy-done.10) | copy-start | bytes 589828
  219.7 9.0 %copy-start.15 = (f32[96,512]{1,0:T(8,128)S(1)}, f32[96,512]{1,0:T(8,128)}, u32[]{:S(2)}) copy-start(f32[96,512]{1,0:T(8,128)} %copy-done.13) | copy-start | bytes 589828
  219.7 9.0 %copy-start.18 = (f32[96,512]{1,0:T(8,128)S(1)}, f32[96,512]{1,0:T(8,128)}, u32[]{:S(2)}) copy-start(f32[96,512]{1,0:T(8,128)} %copy-done.16) | copy-start | bytes 589828
  219.7 9.0 %copy-start.28 = (f32[96,512]{1,0:T(8,128)S(1)}, f32[96,512]{1,0:T(8,128)}, u32[]{:S(2)}) copy-start(f32[96,512]{1,0:T(8,128)} %copy-done.27) | copy-start | bytes 589828
  219.7 9.0 %copy-start.30 = (f32[96,512]{1,0:T(8,128)S(1)}, f32[96,512]{1,0:T(8,128)}, u32[]{:S(2)}) copy-start(f32[96,512]{1,0:T(8,128)} %copy-done.29) | copy-start | bytes 589828
  222.3 35.7 %all-to-all-start.1 = ((f32[32,17,288]{2,1,0:T(8,128)}), f32[32,17,288]{2,1,0:T(8,128)S(1)}, u32[]{:S(2)}, u32[]{:S(2)}) async-start(f32[32,17,288]{2,1,0:T(8,128)} %fusion.9), calls=%async_computation.1 | async-start | bytes 2359296 | tf_op jit(solution)/shard_map/all_to_all | solution.py:318
  233.9 28.4 %copy-start.6 = (f32[3,3,96,512]{3,2,1,0:T(8,128)S(1)}, f32[3,3,96,512]{3,2,1,0:T(8,128)}, u32[]{:S(2)}) copy-start(f32[3,3,96,512]{3,2,1,0:T(8,128)} %fusion.8) | copy-start | bytes 5308420
  269.0 62.6 %copy-start.64 = (f32[1,512]{1,0:T(1,128)S(1)}, f32[1,512]{1,0:T(1,128)}, u32[]{:S(2)}) copy-start(f32[1,512]{1,0:T(1,128)} %param.26) | copy-start | bytes 6148
  (46 other events, 143.9 us)
